TPU v7x, 128 devices: a whole 4x4x4 slice. The times are simulated.
128 devices in a mesh: fsdp: 8 (over z_hi, y), tp: 16 (over z_lo, x, core).
Axes of the slice: x: 4, y: 4, z: 4 (z_hi: 2, z_lo: 2; z = z_hi * 2 + z_lo), core: 2. Of those that a mesh axis runs over, the one named last changes fastest.
Arguments:
- tokens: bfloat16 [2048, 8192], P('fsdp', 'tp'), may hold values from -6 to 6
- out_grad: bfloat16 [2048, 8192], P('fsdp', 'tp'), may hold values from -6 to 6
- gate_weight: bfloat16 [8192, 2048], P('fsdp', 'tp'), may hold values from -0.0625 to 0.0625
- up_weight: bfloat16 [8192, 2048], P('fsdp', 'tp'), may hold values from -0.0625 to 0.0625
- down_weight: bfloat16 [2048, 8192], P('tp', 'fsdp'), may hold values from -0.125 to 0.125
Outputs:
- input_grad: bfloat16 [2048, 8192], P('fsdp', 'tp')
- gate_grad: float32 [8192, 2048], P('fsdp', 'tp')
- up_grad: float32 [8192, 2048], P('fsdp', 'tp')
- down_grad: float32 [2048, 8192], P('tp', 'fsdp')
All inputs are finite; a program needn't handle non-finite values.
Results may differ from a plain program's by a relative error of at most 0.0023.
Values may be sent and summed in bfloat16 or wider, within the bound.
No kernel may reach another device: no remote copies, remote signals or barrier semaphores. Data moves between devices by JAX's collectives and lax.ppermute only.
A program may use at most 128 MiB of HBM per device.

v0:
```python
import math
import jax
import jax.numpy as jnp
from jax import lax
from jax.sharding import Mesh
from jax.sharding import PartitionSpec as P

FSDP = ("fsdp_0", "fsdp_1")


def laid_out(parts, dim):
    parts = jnp.moveaxis(parts, 0, dim)
    dims = parts.shape
    return parts.reshape(*dims[:dim], dims[dim] * dims[dim + 1], *dims[dim + 2 :])


def one_gather(arrays, axis, dims):
    line = jnp.concatenate([a.reshape(-1) for a in arrays])
    lines, at, outs = (lax.all_gather(line, axis), 0, [])
    for a, dim in zip(arrays, dims):
        parts = lines[:, at : at + a.size].reshape(-1, *a.shape)
        outs.append(laid_out(parts, dim))
        at += a.size
    return tuple(outs)


def stacked_from(value, axes, turns):
    parts = value[None]
    for k in turns:
        parts = lax.all_gather(parts, axes[k], axis=0, tiled=True)
    current = [lax.axis_size(axes[k]) for k in reversed(turns)]
    parts = parts.reshape(*current, *value.shape)
    turned = sorted(range(len(turns)), key=lambda place: turns[len(turns) - 1 - place])
    return parts.transpose(*turned, *range(len(turns), parts.ndim)).reshape(-1, *value.shape)


def gathered_by_axis(value, axes, turns, dim):
    return laid_out(stacked_from(value, axes, turns), dim)


def taken_in(value, axes, turns, dim, absorb, carry):
    everything = jax.tree.map(lambda part: gathered_by_axis(part, axes, turns, dim), value)
    return absorb(carry, everything, jnp.int32(0))


def own_rows(portion, rows, axis):
    count = rows * lax.axis_size(axis)
    return lax.psum_scatter(portion(jnp.int32(0), count), axis, scatter_dimension=0, tiled=True)


def column_term(left, right, start, count, factor):
    block = lax.dynamic_slice_in_dim(left, start, count, 1)
    product = lax.dot_general(
        block, right, (((0,), (0,)), ((), ())), preferred_element_type=jnp.float32
    )
    return product * factor


def shards(tokens, out_grad, gate_weight, up_weight, down_weight):
    factor = 1.0 / math.sqrt(tokens.shape[0] * lax.axis_size(FSDP))
    whole = lax.all_gather(tokens, "tp", axis=1, tiled=True)
    grads = lax.all_gather(out_grad, "tp", axis=1, tiled=True)
    gate_full, up_full = one_gather((gate_weight, up_weight), FSDP, (0, 0))
    gate = jnp.dot(whole, gate_full, preferred_element_type=jnp.float32)
    up = jnp.dot(whole, up_full, preferred_element_type=jnp.float32)

    def add_down(total, piece, start):
        columns = lax.dynamic_slice_in_dim(grads, start, piece.shape[1], 1)
        return total + lax.dot_general(
            columns, piece, (((1,), (1,)), ((), ())), preferred_element_type=jnp.float32
        )

    initial = jnp.zeros((whole.shape[0], down_weight.shape[0]), jnp.float32)
    hidden_grad = taken_in(down_weight, FSDP, (0, 1), 1, add_down, initial)
    squashed = jax.nn.sigmoid(gate)
    activated = gate * squashed
    slope = squashed * (1.0 + gate * (1.0 - squashed))
    hidden = (activated * up).astype(jnp.bfloat16)
    gate_delta = (hidden_grad * up * slope).astype(jnp.bfloat16)
    up_delta = (hidden_grad * activated).astype(jnp.bfloat16)

    def rows_term(start, count):
        gate_rows = lax.dynamic_slice_in_dim(gate_full, start, count, 0)
        up_rows = lax.dynamic_slice_in_dim(up_full, start, count, 0)
        first = lax.dot_general(
            gate_rows, gate_delta, (((1,), (1,)), ((), ())), preferred_element_type=jnp.float32
        )
        second = lax.dot_general(
            up_rows, up_delta, (((1,), (1,)), ((), ())), preferred_element_type=jnp.float32
        )
        return first + second

    local_rows = own_rows(rows_term, tokens.shape[1], "tp")
    input_grad = local_rows.T.astype(jnp.bfloat16)
    rows_here = gate_weight.shape[0]

    def joint_term(start, count):
        return jnp.concatenate(
            [
                column_term(whole, gate_delta, start, count, factor),
                column_term(whole, up_delta, start, count, factor),
                column_term(grads, hidden, start, count, factor),
            ],
            axis=1,
        )

    summed = own_rows(joint_term, rows_here, FSDP)
    width = gate_delta.shape[1]
    gate_grad = summed[:, :width]
    up_grad = summed[:, width : 2 * width]
    down_grad = summed[:, 2 * width :].T
    return (input_grad, gate_grad, up_grad, down_grad)


def solution(mesh):
    finer = Mesh(mesh.devices.reshape(2, 4, mesh.shape["tp"]), ("fsdp_0", "fsdp_1", "tp"))
    return jax.shard_map(
        shards,
        mesh=finer,
        in_specs=(P(FSDP, "tp"), P(FSDP, "tp"), P(FSDP, "tp"), P(FSDP, "tp"), P("tp", FSDP)),
        out_specs=(P(FSDP, "tp"), P(FSDP, "tp"), P(FSDP, "tp"), P("tp", FSDP)),
        check_vma=False,
    )
```

profile of v0, /device:TPU:0, one launch (start us, length us, event | category | flops | bytes accessed | tf_op | source)
XLA Modules:
  0.0 450.9 jit_solution(1478735136044264735)
XLA Ops:
  7.2 12.9 %all-gather.1 = bf16[256,1024]{1,0:T(8,128)(2,1)} all-gather(bf16[128,1024]{1,0:T(8,128)(2,1)} %param.9), channel_id=3, replica_groups=mesh['fsdp_0'=2,'fsdp_1'=4,'tp'=16] {'fsdp_0'}, dimensions={0}, use_global_device_ids=true | all-gather | bytes 786432 | tf_op jit(solution)/shard_map/all_gather | solution.py:30
  20.2 1.9 pad_maximum_fusion.1
  23.5 27.7 %all-gather.9.cloned.1.call-done = bf16[8,128,1024]{2,1,0:T(8,128)(2,1)} async-done(((bf16[2,128,1024]{2,1,0:T(8,128)(2,1)}), bf16[8,128,1024]{2,1,0:T(8,128)(2,1)}) %all-gather.9.cloned.1.call-update) | async-done | bytes 2097168 | tf_op jit(solution)/shard_map/all_gather | solution.py:30
  51.2 1.9 copy.27
  53.1 2.4 copy.28
  55.5 70.3 %all-gather.13.cloned.1.call-done = bf16[2097152]{0:T(1024)(128)(2,1)} async-done(((bf16[262144]{0:T(1024)(128)(2,1)}), bf16[2097152]{0:T(1024)(128)(2,1)}) %all-gather.13.cloned.1.call-update) | async-done | bytes 4194320 | tf_op jit(solution)/shard_map/all_gather | solution.py:19
  125.8 5.9 %reshape.28 = bf16[8,262144]{1,0:T(8,128)(2,1)} reshape(bf16[2097152]{0:T(1024)(128)(2,1)} %all-gather.13.cloned.1.call-done) | data formatting | bytes 8388608 | tf_op jit(solution)/shard_map/all_gather | solution.py:19
  131.7 3.9 fusion.6
  135.6 2.3 reshape_reshape.6
  137.9 2.6 reshape_reshape.7
  140.4 21.9 %all-gather.11.cloned.1.call-done = bf16[256,8192]{1,0:T(8,128)(2,1)} async-done(((bf16[256,512]{1,0:T(8,128)(2,1)}), bf16[256,8192]{1,0:T(8,128)(2,1)}) %all-gather.11.cloned.1.call-update) | async-done | bytes 4194320 | tf_op jit(solution)/shard_map/all_gather | solution.py:61
  162.3 4.2 convolution_bitcast_fusion
  166.6 1.3 convolution_bitcast_fusion.1
  167.9 33.2 %all-gather.7.cloned.1.call-done = bf16[256,8192]{1,0:T(8,128)(2,1)} async-done(((bf16[256,512]{1,0:T(8,128)(2,1)}), bf16[256,8192]{1,0:T(8,128)(2,1)}) %all-gather.7.cloned.1.call-update) | async-done | bytes 4194320 | tf_op jit(solution)/shard_map/all_gather | solution.py:62
  201.1 4.2 multiply_convert_fusion.1
  205.4 1.3 fusion.7
  206.6 4.5 convolution_add_fusion
  211.4 3.3 fusion.1
  215.8 1.3 copy-done.3
  218.0 5.0 %pad_maximum_fusion = f32[8192,384]{0,1:T(8,128)} fusion(f32[8192,128]{0,1:T(8,128)S(1)} %fusion, f32[8192,128]{0,1:T(8,128)S(1)} %fusion.1, f32[8192,128]{0,1:T(8,128)S(1)} %fusion.2), kind=kLoop, calls=%fused_computation | loop fusion | flops 6291456 | bytes 25165824 | tf_op jit(solution)/shard_map/concatenate | solution.py:98
  223.0 63.3 %reduce-scatter.3.cloned.1.call-done = f32[512,256]{1,0:T(8,128)} async-done(((f32[8192,256]{1,0:T(8,128)}), f32[512,256]{1,0:T(8,128)}) %reduce-scatter.3.cloned.1.call-update) | async-done | bytes 524304 | tf_op jit(solution)/shard_map/reduce_scatter | solution.py:48
  286.3 1.1 convert_bitcast_fusion
  288.2 151.6 %reduce-scatter.5.cloned.1.call-done = f32[1024,384]{0,1:T(8,128)} async-done(((f32[8192,384]{0,1:T(8,128)}), f32[1024,384]{0,1:T(8,128)}) %reduce-scatter.5.cloned.1.call-update) | async-done | bytes 1572880 | tf_op jit(solution)/shard_map/reduce_scatter | solution.py:48
  439.8 2.3 slice_bitcast_fusion
  (24 shorter events, 6.6 us)
Async XLA Ops:
  7.2 44.0 %all-gather.9.cloned.1.call-start = ((), (), s32[]{:S(2)}) async-start(), calls=%async_computation.3 | async-start | bytes 2621440 | tf_op jit(solution)/shard_map/all_gather | solution.py:30
  20.2 105.7 %all-gather.13.cloned.1.call-start = ((), (), s32[]{:S(2)}) async-start(), calls=%async_computation.7 | async-start | bytes 4718592 | tf_op jit(solution)/shard_map/all_gather | solution.py:19
  22.1 140.2 %all-gather.11.cloned.1.call-start = ((), (), s32[]{:S(2)}) async-start(), calls=%async_computation.4 | async-start | bytes 4456448 | tf_op jit(solution)/shard_map/all_gather | solution.py:61
  22.8 178.3 %all-gather.7.cloned.1.call-start = ((), (), s32[]{:S(2)}) async-start(), calls=%async_computation.2 | async-start | bytes 4456448 | tf_op jit(solution)/shard_map/all_gather | solution.py:62
  23.4 262.9 %reduce-scatter.3.cloned.1.call-start = ((), (), s32[]{:S(2)}) async-start(), calls=%async_computation.5 | async-start | bytes 8912896 | tf_op jit(solution)/shard_map/reduce_scatter | solution.py:48
  162.3 4.2 copy-start
  201.1 4.3 copy-start.2
  211.2 228.6 %reduce-scatter.5.cloned.1.call-start = ((), (), s32[]{:S(2)}) async-start(), calls=%async_computation.6 | async-start | bytes 14155776 | tf_op jit(solution)/shard_map/reduce_scatter | solution.py:48
  211.4 3.5 copy-start.1
  214.8 2.2 copy-start.3
Sparse Core Ops, SparseCore 0:
  20.3 30.8 all-gather.8
  54.1 71.6 all-gather.12
  127.5 34.7 all-gather.10
  163.9 37.2 all-gather.6
  211.3 75.0 reduce-scatter.2
  290.1 149.6 reduce-scatter.4
where the time goes:
time: 451 us
  waiting for transfers between devices  369 us (82%)
  local copies, waits for them, and re-layouts  25.4 us (6%)
  matrix products  20.7 us (5%)
  between operations  14.2 us (3%)
  blocking collectives  12.9 us (3%)
  other arithmetic  7.91 us (2%)
    reduce_scatter x2, waiting for transfers between devices, own_rows(): lax.psum_scatter(portion(jnp.int32(0), count), axis, scatter_dimension=0,...  215 us
    all_gather x1, waiting for transfers between devices, one_gather(): lines, at, outs = (lax.all_gather(line, axis), 0, [])  70.3 us
    all_gather x1, waiting for transfers between devices, shards(): grads = lax.all_gather(out_grad, 'tp', axis=1, tiled=True)  33.2 us
    all_gather x1, waiting for transfers between devices, stacked_from(): parts = lax.all_gather(parts, axes[k], axis=0, tiled=True)  27.7 us
    all_gather x1, waiting for transfers between devices, shards(): whole = lax.all_gather(tokens, 'tp', axis=1, tiled=True)  21.9 us
    all_gather x1, blocking collectives, stacked_from(): parts = lax.all_gather(parts, axes[k], axis=0, tiled=True)  12.9 us
  transfers between devices with their start and end apart: 6, of which 6 were waited for; matrix products, arithmetic and copies ran while one was open for 9% of the time, Pallas kernels for 0%

commit v1 on v0

--- a/solution.py
+++ b/solution.py
@@ -59,7 +59,9 @@
 def shards(tokens, out_grad, gate_weight, up_weight, down_weight):
     factor = 1.0 / math.sqrt(tokens.shape[0] * lax.axis_size(FSDP))
     whole = lax.all_gather(tokens, "tp", axis=1, tiled=True)
-    grads = lax.all_gather(out_grad, "tp", axis=1, tiled=True)
+    grads = jnp.concatenate(
+        lax.all_to_all(jnp.stack([out_grad] * lax.axis_size("tp")), "tp", 0, 0), axis=1
+    )
     gate_full, up_full = one_gather((gate_weight, up_weight), FSDP, (0, 0))
     gate = jnp.dot(whole, gate_full, preferred_element_type=jnp.float32)
     up = jnp.dot(whole, up_full, preferred_element_type=jnp.float32)

time: 451 us -> 432 us (0.958)
  waiting for transfers between devices: 369 us -> 340 us
  starting transfers between devices: 0.42 us -> 5.29 us
    all_gather x1 -> x0, waiting for transfers between devices: 33.2 us -> none  [shards(): grads = lax.all_gather(out_grad, 'tp', axis=1, tiled=True)]
    all_gather x1, waiting for transfers between devices: 70.3 us -> 84.2 us  [one_gather(): lines, at, outs = (lax.all_gather(line, axis), 0, [])]
    all_gather x1, waiting for transfers between devices: 27.7 us -> 19.9 us  [stacked_from(): parts = lax.all_gather(parts, axes[k], axis=0, tiled=True)]
    all_to_all x0 -> x1, starting transfers between devices: none -> 4.91 us  [shards(): lax.all_to_all(jnp.stack([out_grad] * lax.axis_size('tp')), 'tp', 0, 0)]
  transfers between devices with their start and end apart: 6 -> 6, of which waited for: 6 -> 5; matrix products, arithmetic and copies ran while one was open for 9% -> 10% of each run, Pallas kernels for 0% -> 0%
where the time goes in v1:
time: 432 us; the launch traced here: 431 us
  waiting for transfers between devices  340 us (79%)
  local copies, waits for them, and re-layouts  27.6 us (6%)
  matrix products  23.5 us (5%)
  between operations  13.9 us (3%)
  blocking collectives  12.9 us (3%)
  other arithmetic  7.89 us (2%)
  starting transfers between devices  5.29 us (1%)
    reduce_scatter x2, waiting for transfers between devices, own_rows(): lax.psum_scatter(portion(jnp.int32(0), count), axis, scatter_dimension=0,...  213 us
    all_gather x1, waiting for transfers between devices, one_gather(): lines, at, outs = (lax.all_gather(line, axis), 0, [])  84.2 us
    all_gather x1, waiting for transfers between devices, shards(): whole = lax.all_gather(tokens, 'tp', axis=1, tiled=True)  21.9 us
    all_gather x1, waiting for transfers between devices, stacked_from(): parts = lax.all_gather(parts, axes[k], axis=0, tiled=True)  19.9 us
    all_gather x1, blocking collectives, stacked_from(): parts = lax.all_gather(parts, axes[k], axis=0, tiled=True)  12.9 us
  transfers between devices with their start and end apart: 6, of which 5 were waited for; matrix products, arithmetic and copies ran while one was open for 10% of the time, Pallas kernels for 0%

profile of v1, /device:TPU:0, one launch (start us, length us, event | category | flops | bytes accessed | tf_op | source)
XLA Modules:
  0.0 431.4 jit_solution(13825007666663307642)
XLA Ops:
  7.2 12.9 %all-gather.1 = bf16[256,1024]{1,0:T(8,128)(2,1)} all-gather(bf16[128,1024]{1,0:T(8,128)(2,1)} %param.9), channel_id=3, replica_groups=mesh['fsdp_0'=2,'fsdp_1'=4,'tp'=16] {'fsdp_0'}, dimensions={0}, use_global_device_ids=true | all-gather | bytes 786432 | tf_op jit(solution)/shard_map/all_gather | solution.py:30
  20.2 1.9 pad_maximum_fusion.1
  23.2 2.4 stack.2
  25.6 4.9 %all-to-all-start = ((bf16[16,256,512]{1,2,0:T(8,128)(2,1)}), bf16[16,256,512]{1,2,0:T(8,128)(2,1)}, u32[]{:S(2)}, u32[]{:S(2)}) async-start(bf16[16,256,512]{1,2,0:T(8,128)(2,1)} %stack.2), calls=%async_computation | async-start | bytes 8388608 | tf_op jit(solution)/shard_map/all_to_all | solution.py:63
  31.3 19.9 %all-gather.6.cloned.1.call-done = bf16[8,128,1024]{2,1,0:T(8,128)(2,1)} async-done(((bf16[2,128,1024]{2,1,0:T(8,128)(2,1)}), bf16[8,128,1024]{2,1,0:T(8,128)(2,1)}) %all-gather.6.cloned.1.call-update) | async-done | bytes 2097168 | tf_op jit(solution)/shard_map/all_gather | solution.py:30
  51.2 1.9 copy.30
  53.1 2.4 copy.31
  55.5 84.2 %all-gather.10.cloned.1.call-done = bf16[2097152]{0:T(1024)(128)(2,1)} async-done(((bf16[262144]{0:T(1024)(128)(2,1)}), bf16[2097152]{0:T(1024)(128)(2,1)}) %all-gather.10.cloned.1.call-update) | async-done | bytes 4194320 | tf_op jit(solution)/shard_map/all_gather | solution.py:19
  139.7 5.9 %reshape.38 = bf16[8,262144]{1,0:T(8,128)(2,1)} reshape(bf16[2097152]{0:T(1024)(128)(2,1)} %all-gather.10.cloned.1.call-done) | data formatting | bytes 8388608 | tf_op jit(solution)/shard_map/all_gather | solution.py:19
  145.6 3.8 fusion.6
  149.4 2.3 reshape_reshape.6
  151.7 2.6 reshape_reshape.7
  154.3 21.9 %all-gather.8.cloned.1.call-done = bf16[256,8192]{1,0:T(8,128)(2,1)} async-done(((bf16[256,512]{1,0:T(8,128)(2,1)}), bf16[256,8192]{1,0:T(8,128)(2,1)}) %all-gather.8.cloned.1.call-update) | async-done | bytes 4194320 | tf_op jit(solution)/shard_map/all_gather | solution.py:61
  176.2 4.2 convolution_bitcast_fusion
  180.5 1.3 convolution_bitcast_fusion.1
  181.9 4.3 multiply_convert_fusion.1
  186.2 1.2 fusion.7
  187.4 4.5 %convolution_add_fusion = f32[8192,256]{1,0:T(8,128)} fusion(f32[8192,256]{1,0:T(8,128)S(1)} %fusion.7, bf16[8192,128]{1,0:T(8,128)(2,1)S(1)} %reshape_reshape.7, bf16[256,128]{1,0:T(8,128)(2,1)S(1)} %get-tuple-element.25), kind=kOutput, calls=%fused_computation.1 | convolution fusion | flops 538968064 | bytes 18939904 | tf_op jit(solution)/shard_map/dot_general | solution.py:90
  192.2 3.3 fusion.1
  196.6 3.7 fusion
  200.3 5.0 %pad_maximum_fusion = f32[8192,384]{0,1:T(8,128)} fusion(f32[8192,128]{0,1:T(8,128)S(1)} %fusion, f32[8192,128]{0,1:T(8,128)S(1)} %fusion.1, f32[8192,128]{0,1:T(8,128)S(1)} %fusion.2), kind=kLoop, calls=%fused_computation | loop fusion | flops 6291456 | bytes 25165824 | tf_op jit(solution)/shard_map/concatenate | solution.py:100
  205.3 61.9 %reduce-scatter.3.cloned.1.call-done = f32[512,256]{1,0:T(8,128)} async-done(((f32[8192,256]{1,0:T(8,128)}), f32[512,256]{1,0:T(8,128)}) %reduce-scatter.3.cloned.1.call-update) | async-done | bytes 524304 | tf_op jit(solution)/shard_map/reduce_scatter | solution.py:48
  269.0 151.6 %reduce-scatter.5.cloned.1.call-done = f32[1024,384]{0,1:T(8,128)} async-done(((f32[8192,384]{0,1:T(8,128)}), f32[1024,384]{0,1:T(8,128)}) %reduce-scatter.5.cloned.1.call-update) | async-done | bytes 1572880 | tf_op jit(solution)/shard_map/reduce_scatter | solution.py:48
  420.6 2.3 slice_bitcast_fusion
  (23 shorter events, 7.2 us)
Async XLA Ops:
  7.2 44.0 %all-gather.6.cloned.1.call-start = ((), (), s32[]{:S(2)}) async-start(), calls=%async_computation.3 | async-start | bytes 2621440 | tf_op jit(solution)/shard_map/all_gather | solution.py:30
  20.2 119.5 %all-gather.10.cloned.1.call-start = ((), (), s32[]{:S(2)}) async-start(), calls=%async_computation.7 | async-start | bytes 4718592 | tf_op jit(solution)/shard_map/all_gather | solution.py:19
  25.6 156.3 %all-to-all-start = ((bf16[16,256,512]{1,2,0:T(8,128)(2,1)}), bf16[16,256,512]{1,2,0:T(8,128)(2,1)}, u32[]{:S(2)}, u32[]{:S(2)}) async-start(bf16[16,256,512]{1,2,0:T(8,128)(2,1)} %stack.2), calls=%async_computation | async-start | bytes 8388608 | tf_op jit(solution)/shard_map/all_to_all | solution.py:63
  30.5 145.7 %all-gather.8.cloned.1.call-start = ((), (), s32[]{:S(2)}) async-start(), calls=%async_computation.4 | async-start | bytes 4456448 | tf_op jit(solution)/shard_map/all_gather | solution.py:61
  31.2 235.9 %reduce-scatter.3.cloned.1.call-start = ((), (), s32[]{:S(2)}) async-start(), calls=%async_computation.5 | async-start | bytes 8912896 | tf_op jit(solution)/shard_map/reduce_scatter | solution.py:48
  176.2 4.3 copy-start
  181.8 4.3 %copy-start.2 = (bf16[8192,128]{1,0:T(8,128)(2,1)S(1)}, bf16[8192,128]{1,0:T(8,128)(2,1)}, u32[]{:S(2)}) copy-start(bf16[8192,128]{1,0:T(8,128)(2,1)} %reshape_reshape.6) | copy-start | bytes 6291460
  191.9 228.7 %reduce-scatter.5.cloned.1.call-start = ((), (), s32[]{:S(2)}) async-start(), calls=%async_computation.6 | async-start | bytes 14155776 | tf_op jit(solution)/shard_map/reduce_scatter | solution.py:48
  192.2 3.5 copy-start.1
Sparse Core Ops, SparseCore 0:
  20.3 30.8 all-gather.5
  54.1 85.5 all-gather.9
  141.4 34.7 all-gather.7
  192.1 75.0 reduce-scatter.2
  270.9 149.6 reduce-scatter.4
